TPU v7x, 32 devices: a whole 2x2x4 slice. The times are simulated.
32 devices in a mesh: rep: 8 (over y, x, core), shard: 4 (over z).
Axes of the slice: x: 2, y: 2, z: 4, core: 2. Of those that a mesh axis runs over, the one named last changes fastest.
Arguments:
- teacher_states: bfloat16 [3072, 5120], P('rep'), may hold values from -16 to 16
- student_states: bfloat16 [3072, 3584], P('rep'), may hold values from -16 to 16
- teacher_gain: float32 [5120], replicated, may hold values from 0.25 to 1.75
- student_gain: float32 [3584], replicated, may hold values from 0.25 to 1.75
- teacher_query: bfloat16 [5120, 3072], P('rep', 'shard'), may hold values from -1 to 1
- teacher_key: bfloat16 [5120, 1024], P('rep', 'shard'), may hold values from -1 to 1
- teacher_value: bfloat16 [5120, 1024], P('rep', 'shard'), may hold values from -0.078125 to 0.078125
- teacher_output: bfloat16 [5120, 3072], P('rep', 'shard'), may hold values from -0.109375 to 0.109375
- student_query: bfloat16 [3584, 2048], P('rep', 'shard'), may hold values from -1 to 1
- student_key: bfloat16 [3584, 512], P('rep'), may hold values from -1 to 1
- student_value: bfloat16 [3584, 512], P('rep'), may hold values from -0.09375 to 0.09375
- student_output: bfloat16 [3584, 2048], P('rep', 'shard'), may hold values from -0.125 to 0.125
- projection: bfloat16 [3584, 5120], P('rep', 'shard'), may hold values from -0.09375 to 0.09375
Outputs:
- query_grad: float32 [3584, 2048], P('rep', 'shard')
- output_grad: float32 [3584, 2048], P('rep', 'shard')
All inputs are finite; a program needn't handle non-finite values.
Results may differ from a plain program's by a relative error of at most 0.023.
Values may be sent and summed in bfloat16 or wider, within the bound.
A program may use at most 128 MiB of HBM per device.

v0:
```python
from functools import partial
import math
import jax
import jax.numpy as jnp
from jax import lax
from jax.sharding import PartitionSpec as P

HQ_S = 16
KV_S = 4
HD = 128
theta_base = 1000000.0
norm_epsilon = 1e-06


def rms_scale(states, gain):
    values = states.astype(jnp.float32)
    meansq = jnp.mean(values * values, axis=-1, keepdims=True)
    return (values * lax.rsqrt(meansq + norm_epsilon) * gain).astype(jnp.bfloat16)


def rotate(values, head_dim, turning):
    length = values.shape[0]
    halfway = head_dim // 2
    inverse = theta_base ** (-(jnp.arange(halfway, dtype=jnp.float32) * 2.0 / head_dim))
    angles = jnp.arange(length, dtype=jnp.float32)[:, None] * inverse[None, :]
    cosine = jnp.cos(angles)[:, None, :]
    sine = turning * jnp.sin(angles)[:, None, :]
    split = values.reshape(length, -1, head_dim)
    former = split[..., :halfway]
    latter = split[..., halfway:]
    turned = jnp.concatenate(
        [former * cosine - latter * sine, latter * cosine + former * sine], axis=-1
    )
    return turned.reshape(length, -1)


def attend(query_rot, keys, values, head_dim):
    length = query_rot.shape[0]
    kv_heads = keys.shape[1] // head_dim
    group_size = query_rot.shape[1] // head_dim // kv_heads
    queries = query_rot.astype(jnp.bfloat16).reshape(length, kv_heads, group_size, head_dim)
    key_heads = keys.reshape(length, kv_heads, head_dim)
    value_heads = values.reshape(length, kv_heads, head_dim)
    scores = jnp.einsum(
        "qkgd,skd->kgqs", queries, key_heads, preferred_element_type=jnp.float32
    ) * head_dim ** (-0.5)
    rows_index = jnp.arange(length)[:, None]
    column_index = jnp.arange(length)[None, :]
    scores = jnp.where(rows_index >= column_index, scores, -1e30)
    highest = jnp.max(scores, axis=-1, keepdims=True)
    weights = jnp.exp(scores - highest)
    probs = (weights / jnp.sum(weights, axis=-1, keepdims=True)).astype(jnp.bfloat16)
    mixed = jnp.einsum("kgqs,skd->qkgd", probs, value_heads, preferred_element_type=jnp.float32)
    return mixed.reshape(length, -1)


def teacher_side(states, gain, query_w, key_w, value_w, output_w):
    normed = rms_scale(states, gain)
    queries = rotate(jnp.dot(normed, query_w, preferred_element_type=jnp.float32), HD, 1.0)
    keys = rotate(jnp.dot(normed, key_w, preferred_element_type=jnp.float32), HD, 1.0).astype(
        jnp.bfloat16
    )
    values = jnp.dot(normed, value_w, preferred_element_type=jnp.float32).astype(jnp.bfloat16)
    mixed = attend(queries, keys, values, HD).astype(jnp.bfloat16)
    return jnp.dot(mixed, output_w.T, preferred_element_type=jnp.float32)


def student_side(states, gain, query_w, key_w, value_w, output_w):
    normed = rms_scale(states, gain)
    queries = rotate(jnp.dot(normed, query_w, preferred_element_type=jnp.float32), HD, 1.0)
    keys = rotate(jnp.dot(normed, key_w, preferred_element_type=jnp.float32), HD, 1.0).astype(
        jnp.bfloat16
    )
    values = jnp.dot(normed, value_w, preferred_element_type=jnp.float32).astype(jnp.bfloat16)
    mixed_full, pullback = jax.vjp(partial(attend, keys=keys, values=values, head_dim=HD), queries)
    mixed = mixed_full.astype(jnp.bfloat16)
    partial_out = jnp.dot(mixed, output_w.T, preferred_element_type=jnp.float32)
    return (normed, mixed, pullback, partial_out)


def local(
    teacher_states,
    student_states,
    teacher_gain,
    student_gain,
    teacher_query,
    teacher_key,
    teacher_value,
    teacher_output,
    student_query,
    student_key,
    student_value,
    student_output,
    projection,
):
    shard_index = lax.axis_index("shard")
    length = teacher_states.shape[0]
    local_heads = student_query.shape[1] // HD
    group_size = HQ_S // KV_S
    kv_count = max(local_heads // group_size, 1)
    kv_start = shard_index * local_heads // group_size * HD
    key_slice = lax.dynamic_slice_in_dim(student_key, kv_start, kv_count * HD, 1)
    value_slice = lax.dynamic_slice_in_dim(student_value, kv_start, kv_count * HD, 1)
    gathered = (
        lax.all_gather(teacher_query, "rep", axis=0, tiled=True),
        lax.all_gather(teacher_key, "rep", axis=0, tiled=True),
        lax.all_gather(teacher_value, "rep", axis=0, tiled=True),
        lax.all_gather(teacher_output, "rep", axis=0, tiled=True),
        lax.all_gather(student_query, "rep", axis=0, tiled=True),
        lax.all_gather(key_slice, "rep", axis=0, tiled=True),
        lax.all_gather(value_slice, "rep", axis=0, tiled=True),
        lax.all_gather(student_output, "rep", axis=0, tiled=True),
        lax.all_gather(projection, "rep", axis=0, tiled=True),
    )
    teacher_partial = teacher_side(
        teacher_states, teacher_gain, gathered[0], gathered[1], gathered[2], gathered[3]
    )
    student_weights_full = gathered[4:]
    query_full, key_full, value_full, output_full, column_map = student_weights_full
    normed_s, mixed_s, pullback, student_partial = student_side(
        student_states, student_gain, query_full, key_full, value_full, output_full
    )
    block_width = column_map.shape[1]
    attn_block = lax.psum_scatter(
        teacher_partial.astype(jnp.bfloat16), "shard", scatter_dimension=1, tiled=True
    ).astype(jnp.float32)
    attn_student = lax.psum(student_partial.astype(jnp.bfloat16), "shard").astype(jnp.float32)
    own_states = lax.dynamic_slice_in_dim(teacher_states, shard_index * block_width, block_width, 1)
    teacher_hidden = own_states.astype(jnp.float32) + attn_block
    student_hidden = (student_states.astype(jnp.float32) + attn_student).astype(jnp.bfloat16)
    scaling = 1.0 / math.sqrt(lax.axis_size("rep") * length)
    predicted = jnp.dot(student_hidden, column_map, preferred_element_type=jnp.float32)
    grad_pred = ((predicted - teacher_hidden) * scaling).astype(jnp.bfloat16)
    back_term = jnp.dot(grad_pred, column_map.T, preferred_element_type=jnp.float32)
    grad_hidden = lax.psum(back_term.astype(jnp.bfloat16), "shard")
    grad_mixed = jnp.dot(grad_hidden, output_full, preferred_element_type=jnp.float32)
    grad_rot = pullback(grad_mixed)[0]
    grad_query = rotate(grad_rot, HD, -1.0).astype(jnp.bfloat16)
    out_term = jnp.dot(grad_hidden.T, mixed_s, preferred_element_type=jnp.float32)
    query_term = jnp.dot(normed_s.T, grad_query, preferred_element_type=jnp.float32)
    query_grad, output_grad = (
        lax.psum_scatter(
            query_term.astype(jnp.bfloat16), "rep", scatter_dimension=0, tiled=True
        ).astype(jnp.float32),
        lax.psum_scatter(
            out_term.astype(jnp.bfloat16), "rep", scatter_dimension=0, tiled=True
        ).astype(jnp.float32),
    )
    return (query_grad, output_grad)


def solution(mesh):
    return jax.shard_map(
        local,
        mesh=mesh,
        in_specs=(
            P("rep", None),
            P("rep", None),
            P(),
            P(),
            P("rep", "shard"),
            P("rep", "shard"),
            P("rep", "shard"),
            P("rep", "shard"),
            P("rep", "shard"),
            P("rep", None),
            P("rep", None),
            P("rep", "shard"),
            P("rep", "shard"),
        ),
        out_specs=(P("rep", "shard"), P("rep", "shard")),
        check_vma=False,
    )
```

profile of v0, /device:TPU:0, one launch (start us, length us, event | category | flops | bytes accessed | tf_op | source)
XLA Modules:
  0.0 741.3 jit_solution(9428852129858372439)
XLA Ops:
  7.2 0.7 all-gather.8.cloned.1.call-update
  8.0 0.7 all-gather.10.cloned.1.call-update
  8.7 0.7 all-gather.16.cloned.1.call-update
  11.3 0.9 constant_dynamic-slice_fusion.1
  12.2 13.5 %all_gather.28 = bf16[3584,128]{1,0:T(8,128)(2,1)S(1)} all-gather(bf16[448,128]{1,0:T(8,128)(2,1)S(1)} %constant_dynamic-slice_fusion), channel_id=1, replica_groups=mesh['rep'=8,'shard'=4] {'rep'}, dimensions={0}, use_global_device_ids=true | all-gather | bytes 1032192 | tf_op jit(solution)/shard_map/all_gather | solution.py:110
  25.7 11.7 %all_gather.27 = bf16[3584,128]{1,0:T(8,128)(2,1)S(1)} all-gather(bf16[448,128]{1,0:T(8,128)(2,1)S(1)} %constant_dynamic-slice_fusion.1), channel_id=1, replica_groups=mesh['rep'=8,'shard'=4] {'rep'}, dimensions={0}, use_global_device_ids=true | all-gather | bytes 1032192 | tf_op jit(solution)/shard_map/all_gather | solution.py:111
  38.1 1.1 convolution_bitcast_fusion
  39.7 1.4 broadcast_multiply_fusion
  41.1 0.9 fusion.42
  42.1 5.9 all-gather.8.cloned.1.call-done
  47.9 4.6 fusion.75
  52.5 1.4 reshape.234
  54.6 0.7 fusion.25
  55.8 0.9 convolution_convert_fusion.6
  56.7 27.8 %all-gather.10.cloned.1.call-done = bf16[3584,512]{1,0:T(8,128)(2,1)} async-done(((bf16[448,512]{1,0:T(8,128)(2,1)}), bf16[3584,512]{1,0:T(8,128)(2,1)}) %all-gather.10.cloned.1.call-update) | async-done | bytes 3670032 | tf_op jit(solution)/shard_map/all_gather | solution.py:112
  84.6 5.2 convolution_convert_fusion.4
  89.8 0.7 all-gather.12.cloned.1.call-update
  91.3 3.1 fusion.1
  94.9 21.6 %all-gather.16.cloned.1.call-done = bf16[5120,256]{1,0:T(8,128)(2,1)} async-done(((bf16[640,256]{1,0:T(8,128)(2,1)}), bf16[5120,256]{1,0:T(8,128)(2,1)}) %all-gather.16.cloned.1.call-update) | async-done | bytes 2621456 | tf_op jit(solution)/shard_map/all_gather | solution.py:106
  116.5 4.7 fusion.71
  121.2 0.8 fusion.81
  121.9 1.1 copy.54
  123.0 1.8 copy.55
  124.9 1.9 subtract_convert_fusion.3
  126.8 21.5 %all-gather.14.cloned.1.call-done = bf16[5120,256]{1,0:T(8,128)(2,1)} async-done(((bf16[640,256]{1,0:T(8,128)(2,1)}), bf16[5120,256]{1,0:T(8,128)(2,1)}) %all-gather.14.cloned.1.call-update) | async-done | bytes 2621456 | tf_op jit(solution)/shard_map/all_gather | solution.py:107
  148.2 5.4 convolution_convert_fusion.7
  153.6 48.5 %all-gather.18.cloned.1.call-done = bf16[5120,768]{1,0:T(8,128)(2,1)} async-done(((bf16[640,768]{1,0:T(8,128)(2,1)}), bf16[5120,768]{1,0:T(8,128)(2,1)}) %all-gather.18.cloned.1.call-update) | async-done | bytes 7864336 | tf_op jit(solution)/shard_map/all_gather | solution.py:105
  202.0 8.0 %fusion.69 = f32[384,768]{0,1:T(8,128)S(1)} fusion(bf16[5120,768]{1,0:T(8,128)(2,1)} %all-gather.18.cloned.1.call-done, bf16[384,5120]{1,0:T(8,128)(2,1)} %param.13, f32[5120]{0:T(1024)S(1)} %copy-done.10, f32[384]{0:T(512)S(1)} %copy-done.9), kind=kOutput, calls=%fused_computation.110 | convolution fusion | flops 3027763200 | bytes 12998144 | tf_op jit(solution)/shard_map/dot_general | solution.py:59
  210.3 4.2 fusion.82
  214.5 2.6 fusion.30
  217.1 38.7 %all-gather.20.cloned.1.call-done = bf16[5120,768]{1,0:T(8,128)(2,1)} async-done(((bf16[640,768]{1,0:T(8,128)(2,1)}), bf16[5120,768]{1,0:T(8,128)(2,1)}) %all-gather.20.cloned.1.call-update) | async-done | bytes 7864336 | tf_op jit(solution)/shard_map/all_gather | solution.py:108
  255.9 8.4 %convolution_convert_fusion = bf16[384,5120]{1,0:T(8,128)(2,1)} fusion(bf16[384,768]{0,1:T(8,128)(2,1)S(1)} %bitcast.146, bf16[5120,768]{1,0:T(8,128)(2,1)} %all-gather.20.cloned.1.call-done), kind=kOutput, calls=%fused_computation.9 | convolution fusion | flops 3021864960 | bytes 12386304 | tf_op jit(solution)/shard_map/dot_general | solution.py:65
  264.5 102.1 %all-reduce.3.cloned.1.call-done = bf16[384,3584]{1,0:T(8,128)(2,1)} async-done(((bf16[384,3584]{1,0:T(8,128)(2,1)}), bf16[384,3584]{1,0:T(8,128)(2,1)}) %all-reduce.3.cloned.1.call-update) | async-done | bytes 2752528 | tf_op jit(solution)/shard_map/psum | solution.py:127
  366.6 58.5 %all-gather.12.cloned.1.call-done = bf16[3584,1280]{1,0:T(8,128)(2,1)} async-done(((bf16[448,1280]{1,0:T(8,128)(2,1)}), bf16[3584,1280]{1,0:T(8,128)(2,1)}) %all-gather.12.cloned.1.call-update) | async-done | bytes 9175056 | tf_op jit(solution)/shard_map/all_gather | solution.py:113
  425.1 75.0 %reduce-scatter.4.cloned.1.call-done = bf16[384,1280]{1,0:T(8,128)(2,1)} async-done(((bf16[384,5120]{1,0:T(8,128)(2,1)}), bf16[384,1280]{1,0:T(8,128)(2,1)}) %reduce-scatter.4.cloned.1.call-update) | async-done | bytes 983056 | tf_op jit(solution)/shard_map/reduce_scatter | solution.py:124
  500.1 17.8 %convolution_convert_fusion.3 = bf16[384,3584]{1,0:T(8,128)(2,1)} fusion(bf16[3584,1280]{1,0:T(8,128)(2,1)} %all-gather.12.cloned.1.call-done, bf16[384,3584]{1,0:T(8,128)(2,1)} %param.14, bf16[384,3584]{1,0:T(8,128)(2,1)} %all-reduce.3.cloned.1.call-done, bf16[384,1280]{1,0:T(8,128)(2,1)} %reduce-scatter.4.cloned.1.call-done, ...), kind=kOutput, calls=%fused_computation.12 | convolution fusion | flops 7056261120 | bytes 28573700 | tf_op jit(solution)/shard_map/dot_general | solution.py:134
  518.0 108.9 %all-reduce.5.cloned.1.call-done = bf16[384,3584]{1,0:T(8,128)(2,1)} async-done(((bf16[384,3584]{1,0:T(8,128)(2,1)}), bf16[384,3584]{1,0:T(8,128)(2,1)}) %all-reduce.5.cloned.1.call-update) | async-done | bytes 2752528 | tf_op jit(solution)/shard_map/psum | solution.py:135
  626.8 5.7 convolution_convert_fusion.1
  632.8 5.0 fusion.83
  637.9 0.8 fusion.17
  638.7 1.3 convert_reduce_fusion
  640.1 1.6 fusion.34
  642.3 0.9 copy.40
  643.8 5.1 convolution_convert_fusion.2
  649.0 31.3 %reduce-scatter.8.cloned.1.call-done = bf16[448,512]{1,0:T(8,128)(2,1)} async-done(((bf16[3584,512]{1,0:T(8,128)(2,1)}), bf16[448,512]{1,0:T(8,128)(2,1)}) %reduce-scatter.8.cloned.1.call-update) | async-done | bytes 458768 | tf_op jit(solution)/shard_map/reduce_scatter | solution.py:145
  680.3 2.1 convert_element_type.152
  682.3 49.9 %reduce-scatter.6.cloned.1.call-done = bf16[448,512]{1,0:T(8,128)(2,1)} async-done(((bf16[3584,512]{1,0:T(8,128)(2,1)}), bf16[448,512]{1,0:T(8,128)(2,1)}) %reduce-scatter.6.cloned.1.call-update) | async-done | bytes 458768 | tf_op jit(solution)/shard_map/reduce_scatter | solution.py:142
  732.2 2.1 convert_element_type.150
  (73 shorter events, 7.7 us)
Async XLA Ops:
  7.2 4.1 copy-start
  7.2 40.8 %all-gather.8.cloned.1.call-start = ((), (), s32[]{:S(2)}) async-start(), calls=%async_computation.3 | async-start | bytes 4128768 | tf_op jit(solution)/shard_map/all_gather | solution.py:109
  7.9 76.7 %all-gather.10.cloned.1.call-start = ((), (), s32[]{:S(2)}) async-start(), calls=%async_computation.4 | async-start | bytes 4128768 | tf_op jit(solution)/shard_map/all_gather | solution.py:112
  8.7 28.8 %copy-start.2 = (bf16[384,3584]{1,0:T(8,128)(2,1)S(1)}, bf16[384,3584]{1,0:T(8,128)(2,1)}, u32[]{:S(2)}) copy-start(bf16[384,3584]{1,0:T(8,128)(2,1)} %param.14) | copy-start | bytes 8257540
  8.7 107.8 %all-gather.16.cloned.1.call-start = ((), (), s32[]{:S(2)}) async-start(), calls=%async_computation.8 | async-start | bytes 2949120 | tf_op jit(solution)/shard_map/all_gather | solution.py:106
  9.4 138.8 %all-gather.14.cloned.1.call-start = ((), (), s32[]{:S(2)}) async-start(), calls=%async_computation.7 | async-start | bytes 2949120 | tf_op jit(solution)/shard_map/all_gather | solution.py:107
  10.0 192.1 %all-gather.18.cloned.1.call-start = ((), (), s32[]{:S(2)}) async-start(), calls=%async_computation.9 | async-start | bytes 8847360 | tf_op jit(solution)/shard_map/all_gather | solution.py:105
  10.6 245.3 %all-gather.20.cloned.1.call-start = ((), (), s32[]{:S(2)}) async-start(), calls=%async_computation.10 | async-start | bytes 8847360 | tf_op jit(solution)/shard_map/all_gather | solution.py:108
  11.2 26.9 %copy-start.11 = (f32[3584]{0:T(1024)S(1)}, f32[3584]{0:T(1024)}, u32[]{:S(2)}) copy-start(f32[3584]{0:T(1024)} %param.16) | copy-start | bytes 43012
  11.2 355.4 %all-reduce.3.cloned.1.call-start = ((), (), s32[]{:S(2)}) async-start(), calls=%async_computation.5 | async-start | bytes 5505024 | tf_op jit(solution)/shard_map/psum | solution.py:127
  38.1 9.9 %copy-start.7 = (f32[384]{0:T(512)}, f32[384]{0:T(512)S(1)}, u32[]{:S(2)}) copy-start(f32[384]{0:T(512)S(1)} %add_rsqrt_fusion.1) | copy-start | bytes 4612
  39.7 14.9 %copy-start.5 = (bf16[384,64]{0,1:T(8,128)(2,1)}, bf16[384,64]{0,1:T(8,128)(2,1)S(1)}, u32[]{:S(2)}) copy-start(bf16[384,64]{0,1:T(8,128)(2,1)S(1)} %get-tuple-element.18) | copy-start | bytes 147460
  42.1 13.8 %copy-start.15 = (bf16[384,128,1]{1,0,2:T(8,128)(2,1)}, bf16[384,128,1]{1,0,2:T(8,128)(2,1)S(1)}, u32[]{:S(2)}) copy-start(bf16[384,128,1]{1,0,2:T(8,128)(2,1)S(1)} %fusion.42) | copy-start | bytes 294916
  56.7 33.0 %copy-start.13 = (bf16[128,4,384]{2,0,1:T(8,128)(2,1)}, bf16[128,4,384]{2,0,1:T(8,128)(2,1)S(1)}, u32[]{:S(2)}) copy-start(bf16[128,4,384]{2,0,1:T(8,128)(2,1)S(1)} %convolution_convert_fusion.6) | copy-start | bytes 1179652
  89.8 335.3 %all-gather.12.cloned.1.call-start = ((), (), s32[]{:S(2)}) async-start(), calls=%async_computation.6 | async-start | bytes 10321920 | tf_op jit(solution)/shard_map/all_gather | solution.py:113
  90.5 409.5 %reduce-scatter.4.cloned.1.call-start = ((), (), s32[]{:S(2)}) async-start(), calls=%async_computation.11 | async-start | bytes 4915200 | tf_op jit(solution)/shard_map/reduce_scatter | solution.py:124
  126.7 75.3 %copy-start.9 = (f32[384]{0:T(512)S(1)}, f32[384]{0:T(512)}, u32[]{:S(2)}) copy-start(f32[384]{0:T(512)} %add_rsqrt_fusion) | copy-start | bytes 4612
  126.8 75.3 %copy-start.10 = (f32[5120]{0:T(1024)S(1)}, f32[5120]{0:T(1024)}, u32[]{:S(2)}) copy-start(f32[5120]{0:T(1024)} %param.15) | copy-start | bytes 61444
  264.2 362.6 %all-reduce.5.cloned.1.call-start = ((), (), s32[]{:S(2)}) async-start(), calls=%async_computation.12 | async-start | bytes 5505024 | tf_op jit(solution)/shard_map/psum | solution.py:135
  517.9 108.9 %copy-start.14 = (bf16[128,4,384]{2,0,1:T(8,128)(2,1)S(1)}, bf16[128,4,384]{2,0,1:T(8,128)(2,1)}, u32[]{:S(2)}) copy-start(bf16[128,4,384]{2,0,1:T(8,128)(2,1)} %copy-done.13) | copy-start | bytes 1179652
  517.9 162.4 %reduce-scatter.8.cloned.1.call-start = ((), (), s32[]{:S(2)}) async-start(), calls=%async_computation.14 | async-start | bytes 4128768 | tf_op jit(solution)/shard_map/reduce_scatter | solution.py:145
  632.6 99.6 %reduce-scatter.6.cloned.1.call-start = ((), (), s32[]{:S(2)}) async-start(), calls=%async_computation.13 | async-start | bytes 4128768 | tf_op jit(solution)/shard_map/reduce_scatter | solution.py:142
  632.8 5.0 copy-start.16
  638.7 1.3 copy-start.6
  640.1 1.6 copy-start.4
  641.6 2.2 copy-start.3
  641.6 2.2 copy-start.8
  641.7 2.2 copy-start.12
  648.9 85.3 %copy-start.1 = (bf16[448,512]{1,0:T(8,128)(2,1)S(1)}, bf16[448,512]{1,0:T(8,128)(2,1)}, u32[]{:S(2)}) copy-start(bf16[448,512]{1,0:T(8,128)(2,1)} %param.22) | copy-start | bytes 1376260
Sparse Core Ops, SparseCore 0:
  9.9 38.0 all-gather.7
  49.8 34.6 all-gather.9
  86.5 29.9 all-gather.15
  118.2 29.9 all-gather.13
  150.0 52.0 all-gather.17
  203.8 52.0 all-gather.19
  258.2 108.3 all-reduce.2
  368.5 56.5 all-gather.11
  427.4 72.6 reduce-scatter.3
  518.0 108.7 all-reduce.4
  632.7 47.5 reduce-scatter.7
  683.6 48.5 reduce-scatter.5
where the time goes:
time: 750 us; the launch traced here: 741 us
  waiting for transfers between devices  594 us (79%)
  matrix products  82.6 us (11%)
  blocking collectives  25.2 us (3%)
  other arithmetic  15.1 us (2%)
  between operations  14.8 us (2%)
  local copies, waits for them, and re-layouts  8.35 us (1%)
    psum x1, waiting for transfers between devices, local(): grad_hidden = lax.psum(back_term.astype(jnp.bfloat16), 'shard')  109 us
    psum x1, waiting for transfers between devices, local(): lax.psum(student_partial.astype(jnp.bfloat16), 'shard').astype(jnp.float32)  102 us
    reduce_scatter x1, waiting for transfers between devices, local(): lax.psum_scatter(teacher_partial.astype(jnp.bfloat16), 'shard', scatter_d...  75 us
    all_gather x1, waiting for transfers between devices, local(): lax.all_gather(projection, 'rep', axis=0, tiled=True)  58.5 us
    reduce_scatter x1, waiting for transfers between devices, local(): lax.psum_scatter(query_term.astype(jnp.bfloat16), 'rep', scatter_dimensio...  49.9 us
    all_gather x1, waiting for transfers between devices, local(): lax.all_gather(teacher_query, 'rep', axis=0, tiled=True)  48.5 us
    all_gather x1, waiting for transfers between devices, local(): lax.all_gather(teacher_output, 'rep', axis=0, tiled=True)  38.7 us
    reduce_scatter x1, waiting for transfers between devices, local(): lax.psum_scatter(out_term.astype(jnp.bfloat16), 'rep', scatter_dimension=...  31.3 us
  transfers between devices with their start and end apart: 12, of which 12 were waited for; matrix products, arithmetic and copies ran while one was open for 11% of the time, Pallas kernels for 0%

commit v1 on v0

--- a/solution.py
+++ b/solution.py
@@ -124,7 +124,9 @@
     attn_block = lax.psum_scatter(
         teacher_partial.astype(jnp.bfloat16), "shard", scatter_dimension=1, tiled=True
     ).astype(jnp.float32)
-    attn_student = lax.psum(student_partial.astype(jnp.bfloat16), "shard").astype(jnp.float32)
+    attn_student = jnp.sum(
+        lax.all_gather(student_partial.astype(jnp.bfloat16), "shard"), axis=0
+    ).astype(jnp.float32)
     own_states = lax.dynamic_slice_in_dim(teacher_states, shard_index * block_width, block_width, 1)
     teacher_hidden = own_states.astype(jnp.float32) + attn_block
     student_hidden = (student_states.astype(jnp.float32) + attn_student).astype(jnp.bfloat16)

time: 750 us -> 833 us (1.11)
  waiting for transfers between devices: 594 us -> 667 us
    all_gather x0 -> x1, waiting for transfers between devices: none -> 185 us  [local(): lax.all_gather(student_partial.astype(jnp.bfloat16), 'shard')]
    psum x1 -> x0, waiting for transfers between devices: 102 us -> none  [local(): lax.psum(student_partial.astype(jnp.bfloat16), 'shard').astype(jnp.float32)]
    all_gather x1, waiting for transfers between devices: 58.5 us -> 49.6 us  [local(): lax.all_gather(projection, 'rep', axis=0, tiled=True)]
where the time goes in v1:
time: 833 us; the launch traced here: 824 us
  waiting for transfers between devices  667 us (80%)
  matrix products  84.1 us (10%)
  blocking collectives  25.2 us (3%)
  other arithmetic  23.4 us (3%)
  between operations  14.8 us (2%)
  local copies, waits for them, and re-layouts  8.64 us (1%)
    all_gather x1, waiting for transfers between devices, local(): lax.all_gather(student_partial.astype(jnp.bfloat16), 'shard')  185 us
    psum x1, waiting for transfers between devices, local(): grad_hidden = lax.psum(back_term.astype(jnp.bfloat16), 'shard')  109 us
    reduce_scatter x1, waiting for transfers between devices, local(): lax.psum_scatter(teacher_partial.astype(jnp.bfloat16), 'shard', scatter_d...  75 us
    reduce_scatter x1, waiting for transfers between devices, local(): lax.psum_scatter(query_term.astype(jnp.bfloat16), 'rep', scatter_dimensio...  49.9 us
    all_gather x1, waiting for transfers between devices, local(): lax.all_gather(projection, 'rep', axis=0, tiled=True)  49.6 us
    all_gather x1, waiting for transfers between devices, local(): lax.all_gather(teacher_query, 'rep', axis=0, tiled=True)  48.4 us
    all_gather x1, waiting for transfers between devices, local(): lax.all_gather(teacher_output, 'rep', axis=0, tiled=True)  36.9 us
    reduce_scatter x1, waiting for transfers between devices, local(): lax.psum_scatter(out_term.astype(jnp.bfloat16), 'rep', scatter_dimension=...  31.3 us
  transfers between devices with their start and end apart: 12, of which 12 were waited for; matrix products, arithmetic and copies ran while one was open for 11% of the time, Pallas kernels for 0%

profile of v1, /device:TPU:0, one launch (start us, length us, event | category | flops | bytes accessed | tf_op | source)
XLA Modules:
  0.0 824.0 jit_solution(14518701641345884205)
XLA Ops:
  11.3 0.9 constant_dynamic-slice_fusion.1
  12.2 13.5 %all_gather.34 = bf16[3584,128]{1,0:T(8,128)(2,1)S(1)} all-gather(bf16[448,128]{1,0:T(8,128)(2,1)S(1)} %constant_dynamic-slice_fusion), channel_id=1, replica_groups=mesh['rep'=8,'shard'=4] {'rep'}, dimensions={0}, use_global_device_ids=true | all-gather | bytes 1032192 | tf_op jit(solution)/shard_map/all_gather | solution.py:110
  25.7 11.7 %all_gather.33 = bf16[3584,128]{1,0:T(8,128)(2,1)S(1)} all-gather(bf16[448,128]{1,0:T(8,128)(2,1)S(1)} %constant_dynamic-slice_fusion.1), channel_id=1, replica_groups=mesh['rep'=8,'shard'=4] {'rep'}, dimensions={0}, use_global_device_ids=true | all-gather | bytes 1032192 | tf_op jit(solution)/shard_map/all_gather | solution.py:111
  38.1 1.1 convolution_bitcast_fusion
  39.7 1.4 broadcast_multiply_fusion
  41.1 0.9 fusion.42
  42.1 5.8 all-gather.10.cloned.1.call-done
  47.9 4.5 fusion.75
  52.5 1.4 reshape.234
  54.6 0.7 fusion.25
  55.8 0.9 convolution_convert_fusion.6
  56.7 27.9 %all-gather.12.cloned.1.call-done = bf16[3584,512]{1,0:T(8,128)(2,1)} async-done(((bf16[448,512]{1,0:T(8,128)(2,1)}), bf16[3584,512]{1,0:T(8,128)(2,1)}) %all-gather.12.cloned.1.call-update) | async-done | bytes 3670032 | tf_op jit(solution)/shard_map/all_gather | solution.py:112
  84.6 5.3 convolution_convert_fusion.4
  91.1 0.7 copy.34
  91.9 0.7 copy.35
  92.6 3.1 fusion.1
  95.8 20.7 %all-gather.18.cloned.1.call-done = bf16[5120,256]{1,0:T(8,128)(2,1)} async-done(((bf16[640,256]{1,0:T(8,128)(2,1)}), bf16[5120,256]{1,0:T(8,128)(2,1)}) %all-gather.18.cloned.1.call-update) | async-done | bytes 2621456 | tf_op jit(solution)/shard_map/all_gather | solution.py:106
  116.5 4.7 fusion.71
  121.2 0.7 fusion.81
  121.9 1.1 copy.54
  123.0 0.9 copy.55
  123.9 1.8 subtract_convert_fusion.3
  125.7 22.6 %all-gather.16.cloned.1.call-done = bf16[5120,256]{1,0:T(8,128)(2,1)} async-done(((bf16[640,256]{1,0:T(8,128)(2,1)}), bf16[5120,256]{1,0:T(8,128)(2,1)}) %all-gather.16.cloned.1.call-update) | async-done | bytes 2621456 | tf_op jit(solution)/shard_map/all_gather | solution.py:107
  148.2 5.4 convolution_convert_fusion.7
  153.6 48.4 %all-gather.20.cloned.1.call-done = bf16[5120,768]{1,0:T(8,128)(2,1)} async-done(((bf16[640,768]{1,0:T(8,128)(2,1)}), bf16[5120,768]{1,0:T(8,128)(2,1)}) %all-gather.20.cloned.1.call-update) | async-done | bytes 7864336 | tf_op jit(solution)/shard_map/all_gather | solution.py:105
  202.0 8.0 fusion.69
  210.2 0.9 pad_maximum_fusion
  211.1 4.5 fusion.82
  215.6 3.3 fusion.30
  218.9 36.9 %all-gather.22.cloned.1.call-done = bf16[5120,768]{1,0:T(8,128)(2,1)} async-done(((bf16[640,768]{1,0:T(8,128)(2,1)}), bf16[5120,768]{1,0:T(8,128)(2,1)}) %all-gather.22.cloned.1.call-update) | async-done | bytes 7864336 | tf_op jit(solution)/shard_map/all_gather | solution.py:108
  255.9 8.7 %convolution_convert_fusion = bf16[384,5120]{1,0:T(8,128)(2,1)} fusion(bf16[384,768]{0,1:T(8,128)(2,1)} %bitcast.148, bf16[5120,768]{1,0:T(8,128)(2,1)} %all-gather.22.cloned.1.call-done), kind=kOutput, calls=%fused_computation.9 | convolution fusion | flops 3021864960 | bytes 12386304 | tf_op jit(solution)/shard_map/dot_general | solution.py:65
  264.8 185.1 %all-gather.24.cloned.1.call-done = bf16[1536,3584]{1,0:T(8,128)(2,1)} async-done(((bf16[384,3584]{1,0:T(8,128)(2,1)}), bf16[1536,3584]{1,0:T(8,128)(2,1)}) %all-gather.24.cloned.1.call-update) | async-done | bytes 11010064 | tf_op jit(solution)/shard_map/all_gather | solution.py:128
  449.9 8.1 reduce_sum.85
  458.0 49.6 %all-gather.14.cloned.1.call-done = bf16[3584,1280]{1,0:T(8,128)(2,1)} async-done(((bf16[448,1280]{1,0:T(8,128)(2,1)}), bf16[3584,1280]{1,0:T(8,128)(2,1)}) %all-gather.14.cloned.1.call-update) | async-done | bytes 9175056 | tf_op jit(solution)/shard_map/all_gather | solution.py:113
  507.6 75.0 %reduce-scatter.4.cloned.1.call-done = bf16[384,1280]{1,0:T(8,128)(2,1)} async-done(((bf16[384,5120]{1,0:T(8,128)(2,1)}), bf16[384,1280]{1,0:T(8,128)(2,1)}) %reduce-scatter.4.cloned.1.call-update) | async-done | bytes 983056 | tf_op jit(solution)/shard_map/reduce_scatter | solution.py:124
  582.6 18.0 %convolution_convert_fusion.3 = bf16[384,3584]{1,0:T(8,128)(2,1)} fusion(bf16[3584,1280]{1,0:T(8,128)(2,1)} %all-gather.14.cloned.1.call-done, bf16[384,3584]{1,0:T(8,128)(2,1)} %param.14, bf16[384,3584]{1,0:T(8,128)(2,1)} %reduce_sum.85, bf16[384,1280]{1,0:T(8,128)(2,1)} %reduce-scatter.4.cloned.1.call-done, bf16[384,5120]{1,0:T(8,128)(2,1)} %param.13, ...), kind=kOutput, calls=%fused_computation.12 | convolution fusion | flops 7056261120 | bytes 28573700 | tf_op jit(solution)/shard_map/dot_general | solution.py:136
  600.6 108.9 %all-reduce.2.cloned.1.call-done = bf16[384,3584]{1,0:T(8,128)(2,1)} async-done(((bf16[384,3584]{1,0:T(8,128)(2,1)}), bf16[384,3584]{1,0:T(8,128)(2,1)}) %all-reduce.2.cloned.1.call-update) | async-done | bytes 2752528 | tf_op jit(solution)/shard_map/psum | solution.py:137
  709.5 5.7 convolution_convert_fusion.1
  715.5 5.0 fusion.83
  720.5 0.8 fusion.17
  721.4 1.3 convert_reduce_fusion
  722.7 1.6 fusion.34
  725.0 0.9 copy.40
  726.5 5.1 convolution_convert_fusion.2
  731.6 31.3 %reduce-scatter.8.cloned.1.call-done = bf16[448,512]{1,0:T(8,128)(2,1)} async-done(((bf16[3584,512]{1,0:T(8,128)(2,1)}), bf16[448,512]{1,0:T(8,128)(2,1)}) %reduce-scatter.8.cloned.1.call-update) | async-done | bytes 458768 | tf_op jit(solution)/shard_map/reduce_scatter | solution.py:147
  763.0 2.1 convert_element_type.154
  765.0 49.9 %reduce-scatter.6.cloned.1.call-done = bf16[448,512]{1,0:T(8,128)(2,1)} async-done(((bf16[3584,512]{1,0:T(8,128)(2,1)}), bf16[448,512]{1,0:T(8,128)(2,1)}) %reduce-scatter.6.cloned.1.call-update) | async-done | bytes 458768 | tf_op jit(solution)/shard_map/reduce_scatter | solution.py:144
  814.9 2.1 convert_element_type.152
  (84 shorter events, 9.6 us)
Async XLA Ops:
  7.2 4.1 copy-start
  7.2 40.8 %all-gather.10.cloned.1.call-start = ((), (), s32[]{:S(2)}) async-start(), calls=%async_computation.3 | async-start | bytes 4128768 | tf_op jit(solution)/shard_map/all_gather | solution.py:109
  7.9 76.7 %all-gather.12.cloned.1.call-start = ((), (), s32[]{:S(2)}) async-start(), calls=%async_computation.4 | async-start | bytes 4128768 | tf_op jit(solution)/shard_map/all_gather | solution.py:112
  8.7 28.8 %copy-start.2 = (bf16[384,3584]{1,0:T(8,128)(2,1)S(1)}, bf16[384,3584]{1,0:T(8,128)(2,1)}, u32[]{:S(2)}) copy-start(bf16[384,3584]{1,0:T(8,128)(2,1)} %param.14) | copy-start | bytes 8257540
  8.7 107.8 %all-gather.18.cloned.1.call-start = ((), (), s32[]{:S(2)}) async-start(), calls=%async_computation.7 | async-start | bytes 2949120 | tf_op jit(solution)/shard_map/all_gather | solution.py:106
  9.4 138.8 %all-gather.16.cloned.1.call-start = ((), (), s32[]{:S(2)}) async-start(), calls=%async_computation.6 | async-start | bytes 2949120 | tf_op jit(solution)/shard_map/all_gather | solution.py:107
  10.0 192.1 %all-gather.20.cloned.1.call-start = ((), (), s32[]{:S(2)}) async-start(), calls=%async_computation.8 | async-start | bytes 8847360 | tf_op jit(solution)/shard_map/all_gather | solution.py:105
  10.6 245.3 %all-gather.22.cloned.1.call-start = ((), (), s32[]{:S(2)}) async-start(), calls=%async_computation.9 | async-start | bytes 8847360 | tf_op jit(solution)/shard_map/all_gather | solution.py:108
  11.2 26.9 %copy-start.15 = (f32[3584]{0:T(1024)S(1)}, f32[3584]{0:T(1024)}, u32[]{:S(2)}) copy-start(f32[3584]{0:T(1024)} %param.16) | copy-start | bytes 43012
  11.2 438.8 %all-gather.24.cloned.1.call-start = ((), (), s32[]{:S(2)}) async-start(), calls=%async_computation.14 | async-start | bytes 13762560 | tf_op jit(solution)/shard_map/all_gather | solution.py:128
  38.1 9.9 %copy-start.9 = (f32[384]{0:T(512)}, f32[384]{0:T(512)S(1)}, u32[]{:S(2)}) copy-start(f32[384]{0:T(512)S(1)} %add_rsqrt_fusion.1) | copy-start | bytes 4612
  39.7 14.9 %copy-start.7 = (bf16[384,64]{0,1:T(8,128)(2,1)}, bf16[384,64]{0,1:T(8,128)(2,1)S(1)}, u32[]{:S(2)}) copy-start(bf16[384,64]{0,1:T(8,128)(2,1)S(1)} %get-tuple-element.18) | copy-start | bytes 147460
  42.1 13.7 %copy-start.20 = (bf16[384,128,1]{1,0,2:T(8,128)(2,1)}, bf16[384,128,1]{1,0,2:T(8,128)(2,1)S(1)}, u32[]{:S(2)}) copy-start(bf16[384,128,1]{1,0,2:T(8,128)(2,1)S(1)} %fusion.42) | copy-start | bytes 294916
  56.7 33.1 %copy-start.17 = (bf16[128,4,384]{2,0,1:T(8,128)(2,1)}, bf16[128,4,384]{2,0,1:T(8,128)(2,1)S(1)}, u32[]{:S(2)}) copy-start(bf16[128,4,384]{2,0,1:T(8,128)(2,1)S(1)} %convolution_convert_fusion.6) | copy-start | bytes 1179652
  89.9 26.6 %copy-start.13 = (f32[5120]{0:T(1024)S(1)}, f32[5120]{0:T(1024)}, u32[]{:S(2)}) copy-start(f32[5120]{0:T(1024)} %param.15) | copy-start | bytes 61444
  89.9 417.8 %all-gather.14.cloned.1.call-start = ((), (), s32[]{:S(2)}) async-start(), calls=%async_computation.5 | async-start | bytes 10321920 | tf_op jit(solution)/shard_map/all_gather | solution.py:113
  90.6 492.0 %reduce-scatter.4.cloned.1.call-start = ((), (), s32[]{:S(2)}) async-start(), calls=%async_computation.10 | async-start | bytes 4915200 | tf_op jit(solution)/shard_map/reduce_scatter | solution.py:124
  95.8 25.4 %copy-start.11 = (f32[384]{0:T(512)}, f32[384]{0:T(512)S(1)}, u32[]{:S(2)}) copy-start(f32[384]{0:T(512)S(1)} %add_rsqrt_fusion) | copy-start | bytes 4612
  125.7 76.4 %copy-start.12 = (f32[384]{0:T(512)S(1)}, f32[384]{0:T(512)}, u32[]{:S(2)}) copy-start(f32[384]{0:T(512)} %copy-done.11) | copy-start | bytes 4612
  125.7 76.4 %copy-start.14 = (f32[5120]{0:T(1024)S(1)}, f32[5120]{0:T(1024)}, u32[]{:S(2)}) copy-start(f32[5120]{0:T(1024)} %param.15) | copy-start | bytes 61444
  153.6 56.5 %copy-start.5 = (f32[384,64]{0,1:T(8,128)S(1)}, f32[384,64]{0,1:T(8,128)}, u32[]{:S(2)}) copy-start(f32[384,64]{0,1:T(8,128)} %copy.34) | copy-start | bytes 294916
  153.6 56.5 %copy-start.6 = (f32[384,64]{0,1:T(8,128)S(1)}, f32[384,64]{0,1:T(8,128)}, u32[]{:S(2)}) copy-start(f32[384,64]{0,1:T(8,128)} %copy.35) | copy-start | bytes 294916
  211.1 4.5 copy-start.19
  264.6 444.9 %all-reduce.2.cloned.1.call-start = ((), (), s32[]{:S(2)}) async-start(), calls=%async_computation.11 | async-start | bytes 5505024 | tf_op jit(solution)/shard_map/psum | solution.py:137
  600.6 109.0 %copy-start.18 = (bf16[128,4,384]{2,0,1:T(8,128)(2,1)S(1)}, bf16[128,4,384]{2,0,1:T(8,128)(2,1)}, u32[]{:S(2)}) copy-start(bf16[128,4,384]{2,0,1:T(8,128)(2,1)} %copy-done.17) | copy-start | bytes 1179652
  600.6 162.4 %reduce-scatter.8.cloned.1.call-start = ((), (), s32[]{:S(2)}) async-start(), calls=%async_computation.13 | async-start | bytes 4128768 | tf_op jit(solution)/shard_map/reduce_scatter | solution.py:147
  715.2 99.6 %reduce-scatter.6.cloned.1.call-start = ((), (), s32[]{:S(2)}) async-start(), calls=%async_computation.12 | async-start | bytes 4128768 | tf_op jit(solution)/shard_map/reduce_scatter | solution.py:144
  715.5 5.0 copy-start.21
  721.4 1.3 copy-start.8
  722.7 1.6 copy-start.4
  724.3 2.2 copy-start.3
  724.3 2.2 copy-start.10
  724.3 2.2 copy-start.16
  731.6 85.3 %copy-start.1 = (bf16[448,512]{1,0:T(8,128)(2,1)S(1)}, bf16[448,512]{1,0:T(8,128)(2,1)}, u32[]{:S(2)}) copy-start(bf16[448,512]{1,0:T(8,128)(2,1)} %param.22) | copy-start | bytes 1376260
Sparse Core Ops, SparseCore 0:
  9.9 38.0 all-gather.9
  49.8 34.7 all-gather.11
  86.5 29.9 all-gather.17
  118.2 29.9 all-gather.15
  150.0 52.0 all-gather.19
  203.8 52.0 all-gather.21
  257.4 192.4 all-gather.23
  451.8 55.7 all-gather.13
  509.9 72.6 reduce-scatter.3
  600.7 108.7 all-reduce.1
  715.3 47.5 reduce-scatter.7
  766.3 48.5 reduce-scatter.5
